TPU v7x, 256 devices: a whole 4x4x8 slice. The times are simulated.
256 devices in a mesh: role: 2 (over z_hi), dp: 16 (over y, z_lo), mp: 8 (over x, core).
Axes of the slice: x: 4, y: 4, z: 8 (z_hi: 2, z_lo: 4; z = z_hi * 4 + z_lo), core: 2. Of those that a mesh axis runs over, the one named last changes fastest.
Arguments:
- patches: bfloat16 [25088, 1280], P('dp', 'mp'), may hold values from -6 to 6
- pred_states: bfloat16 [16384, 384], P('dp'), may hold values from -6 to 6
- ema_up: bfloat16 [1280, 5120], P(('role', 'dp'), 'mp'), may hold values from -0.15625 to 0.15625
- ema_down: bfloat16 [5120, 1280], P('mp', ('role', 'dp')), may hold values from -0.078125 to 0.078125
- pred_up: bfloat16 [384, 1536], P(('role', 'dp'), 'mp'), may hold values from -0.3125 to 0.3125
- pred_down: bfloat16 [1536, 384], P('mp', ('role', 'dp')), may hold values from -0.15625 to 0.15625
- pred_out: bfloat16 [384, 1280], P(('role', 'dp'), 'mp'), may hold values from -0.3125 to 0.3125
- masked_index: int32 [16, 1024], P('dp'), may hold values from 0 to 1567, as said below
- masked_count: int32 [16], P('dp'), may hold values from 512 to 1024, as said below
- loss_scale: float32 [], replicated, may hold values from 81920 to 327680
Outputs:
- loss: float32 [], replicated
- grad_up: float32 [384, 1536], P(('role', 'dp'), 'mp')
- grad_down: float32 [1536, 384], P('mp', ('role', 'dp'))
- grad_out: float32 [384, 1280], P(('role', 'dp'), 'mp')
Inputs may be any that keep to these rules, and one draw needn't show every extreme that they name: `masked_index`: within a clip the slots name distinct tokens; the slots below masked_count name the masked tokens, which are whole tubes: all 8 frames (token f * 196 + s for frame f) of some spatial positions s. Slots from masked_count on name other tokens and are ignored. `masked_count`: each count is 8 times a whole number; some clip has exactly 1024.
All inputs are finite; a program needn't handle non-finite values.
Results may differ from a plain program's by a relative error of at most 0.012.
Values may be sent and summed in bfloat16 or wider, within the bound.
No kernel may reach another device: no remote copies, remote signals or barrier semaphores. Data moves between devices by JAX's collectives and lax.ppermute only.
A program may use at most 128 MiB of HBM per device.

v0:
```python
import functools

import jax
import jax.numpy as jnp
from jax import lax
from jax.sharding import Mesh
from jax.sharding import PartitionSpec as P

D = 1280
TOK = 1568
MMAX = 1024
MP = ("mp_0", "mp_1")
ROLE_DP = ("role", "dp_0", "dp_1")
DP = ("dp_0", "dp_1")
ROLE_DP_MP = ("role", "dp_0", "dp_1", "mp_0", "mp_1")


EPS = 1e-06
COEF = 0.7978845608028654


def joined_along(pieces, dim):
    pieces = jnp.moveaxis(pieces, 0, dim)
    lengths = pieces.shape
    return pieces.reshape(*lengths[:dim], lengths[dim] * lengths[dim + 1], *lengths[dim + 2 :])


def from_everyone(shard, axis):
    copies = jnp.broadcast_to(shard, (lax.axis_size(axis), *shard.shape))
    return lax.all_to_all(copies, axis, split_axis=0, concat_axis=0, tiled=True)


def gather_directly(shard, axis, dim):
    return joined_along(from_everyone(shard, axis), dim)


def of_everyone(shard, axis):
    return from_everyone(shard, axis).sum(axis=0)


def in_one(arrays, axis):
    vector, at, outs = (jnp.concatenate([a.reshape(-1) for a in arrays]), 0, [])
    total = of_everyone(vector, axis)
    for a in arrays:
        outs.append(total[at : at + a.size].reshape(a.shape))
        at += a.size
    return tuple(outs)


def passed_along(block, axis, distance):
    devices = range(lax.axis_size(axis))
    route = [(i - distance, i) for i in devices if i - distance in devices]
    return lax.ppermute(block, axis, route)


def sent_together(arrays, axis, dim, along):
    widths = [a.shape[along] for a in arrays]
    both = jnp.concatenate(arrays, axis=along)
    filled = lax.all_gather(both, axis, axis=dim, tiled=True)
    return tuple(jnp.split(filled, [sum(widths[:k]) for k in range(1, len(widths))], axis=along))


def by_axis(shard, axes):
    return functools.reduce(lax.psum, axes, shard)


def filled_up(lines, devices):
    spare = -len(lines) % devices
    return jnp.pad(lines, [(0, spare)] + [(0, 0)] * (lines.ndim - 1))


def sum_by_parts(shard, axis):
    lines = shard.reshape(-1, *shard.shape[1:][-1:])
    own = lax.psum_scatter(
        filled_up(lines, lax.axis_size(axis)), axis, scatter_dimension=0, tiled=True
    )
    whole = lax.all_gather(own, axis).reshape(-1, *lines.shape[1:])
    return lax.slice_in_dim(whole, 0, len(lines)).reshape(shard.shape)


def cut_along(shard, dim, devices):
    before, after = (shard.shape[:dim], shard.shape[dim + 1 :])
    return jnp.moveaxis(shard.reshape(*before, devices, -1, *after), dim, 0)


def sum_together(arrays, axis, dims):
    devices = lax.axis_size(axis)
    pieces = [cut_along(a, dim, devices) for a, dim in zip(arrays, dims)]
    lines = jnp.concatenate([b.reshape(devices, -1) for b in pieces], axis=1)
    width = max(16, -(-lines.shape[1] // 1024) * 8)
    lines = jnp.pad(lines, ((0, 0), (0, width * 128 - lines.shape[1]))).reshape(-1, 128)
    vector, at, outs = (lax.psum_scatter(lines, axis, tiled=True).reshape(-1), 0, [])
    for b in pieces:
        part = b[0]
        outs.append(vector[at : at + part.size].reshape(part.shape))
        at += part.size
    return tuple(outs)


def summed_on_arrival(shard, axis, dim):
    pieces = cut_along(shard, dim, lax.axis_size(axis))
    arrived = lax.all_to_all(pieces, axis, split_axis=0, concat_axis=0, tiled=True)
    return arrived.sum(axis=0)


def normalize(values):
    row_mean = jnp.mean(values, axis=-1, keepdims=True)
    row_deviations = values - row_mean
    variance = jnp.mean(row_deviations * row_deviations, axis=-1, keepdims=True)
    return row_deviations * lax.rsqrt(variance + EPS)


def gelu_slope(values):
    inner = COEF * (values + 0.044715 * values * values * values)
    tangent = jnp.tanh(inner)
    return 0.5 * (1.0 + tangent) + 0.5 * values * (1.0 - tangent * tangent) * COEF * (
        1.0 + 3.0 * 0.044715 * values * values
    )


def pick_rows(source_table, token_index):
    clip_count = token_index.shape[0]
    slot_total = token_index.shape[1]
    clip_grid = source_table.reshape(clip_count, TOK, source_table.shape[1])
    onehot = (token_index[:, :, None] == jnp.arange(TOK, dtype=jnp.int32)[None, None, :]).astype(
        jnp.bfloat16
    )
    picked = jnp.einsum("ckt,ctw->ckw", onehot, clip_grid, preferred_element_type=jnp.float32)
    return picked.astype(jnp.bfloat16).reshape(clip_count * slot_total, source_table.shape[1])


def body(
    patches,
    pred_states,
    ema_up,
    ema_down,
    pred_up,
    pred_down,
    pred_out,
    masked_index,
    masked_count,
    loss_scale,
):
    role_index = lax.axis_index("role")
    clip_count = masked_index.shape[0]
    feat_width = float(D)
    half_slots = MMAX // 2
    half_index = lax.dynamic_slice_in_dim(masked_index, role_index * half_slots, half_slots, 1)
    own_rows = pick_rows(patches, half_index)
    whole_rows = gather_directly(own_rows, MP, 1)
    working = role_index >= 0
    block_rows = own_rows.shape[0]
    up_cols = lax.all_gather(ema_up, ROLE_DP, axis=0, tiled=True)
    down_rows = lax.all_gather(ema_down, ROLE_DP, axis=1, tiled=True)

    def encode_block():
        normed = normalize(whole_rows.astype(jnp.float32)).astype(jnp.bfloat16)
        hidden = jax.nn.gelu(
            jnp.dot(normed, up_cols, preferred_element_type=jnp.float32), approximate=True
        ).astype(jnp.bfloat16)
        return jnp.dot(hidden, down_rows, preferred_element_type=jnp.float32)

    def skip_block():
        return jnp.zeros((block_rows, whole_rows.shape[1]), jnp.float32)

    partial_sum = lax.cond(working, encode_block, skip_block)
    branch = lax.psum_scatter(partial_sum, MP, scatter_dimension=1, tiled=True)
    block_out = own_rows.astype(jnp.float32) + branch
    first_sum, second_sum = in_one(
        (
            jnp.sum(block_out, axis=-1, keepdims=True),
            jnp.sum(block_out * block_out, axis=-1, keepdims=True),
        ),
        MP,
    )
    row_mean = first_sum / feat_width
    row_deviations = block_out - row_mean
    variance = second_sum / feat_width - row_mean * row_mean
    target_all = (row_deviations * lax.rsqrt(variance + EPS)).astype(jnp.bfloat16)
    local_width = target_all.shape[1]
    earlier = passed_along(target_all, "role", 1)
    joined = jnp.concatenate(
        (
            earlier.reshape(clip_count, half_slots, local_width),
            target_all.reshape(clip_count, half_slots, local_width),
        ),
        axis=1,
    )
    targets = joined.reshape(clip_count * MMAX, local_width)
    up_rows, out_rows = sent_together((pred_up, pred_out), ROLE_DP, 0, 1)
    down_cols = gather_directly(pred_down, ROLE_DP, 1)
    total = of_everyone(jnp.sum(masked_count).astype(jnp.float32), DP)
    states = pred_states.astype(jnp.float32)
    pnormed = normalize(states).astype(jnp.bfloat16)
    preact = jnp.dot(pnormed, up_rows, preferred_element_type=jnp.float32)
    hid_act = jax.nn.gelu(preact, approximate=True).astype(jnp.bfloat16)
    mixer_out = lax.psum(jnp.dot(hid_act, down_cols, preferred_element_type=jnp.float32), MP)
    updated = states + mixer_out
    row_mean_p = jnp.mean(updated, axis=-1, keepdims=True)
    predictor_deviations = updated - row_mean_p
    reciprocal_spread = lax.rsqrt(
        jnp.mean(predictor_deviations * predictor_deviations, axis=-1, keepdims=True) + EPS
    )
    standardized_input = predictor_deviations * reciprocal_spread
    output_normalized = standardized_input.astype(jnp.bfloat16)
    predicted = jnp.dot(output_normalized, out_rows, preferred_element_type=jnp.float32)
    live_mask = (
        (jnp.arange(MMAX, dtype=jnp.int32)[None, :] < masked_count[:, None])
        .astype(jnp.float32)
        .reshape(clip_count * MMAX, 1)
    )
    predictor_side = (role_index == 1).astype(jnp.float32)
    norm_scale = total * feat_width
    residue = predicted - targets.astype(jnp.float32)
    smooth = jnp.sqrt(residue * residue + 1.0)
    local_loss = jnp.sum(live_mask * (smooth - 1.0)) * predictor_side
    loss = by_axis(local_loss, ROLE_DP_MP) / norm_scale
    grad_pred = (loss_scale * live_mask * residue / smooth / norm_scale * predictor_side).astype(
        jnp.bfloat16
    )
    normalized_gradient = sum_by_parts(
        jnp.einsum("rd,kd->rk", grad_pred, out_rows, preferred_element_type=jnp.float32), MP
    )
    gradient_update = reciprocal_spread * (
        normalized_gradient
        - jnp.mean(normalized_gradient, axis=-1, keepdims=True)
        - standardized_input
        * jnp.mean(normalized_gradient * standardized_input, axis=-1, keepdims=True)
    )
    gradient_update = gradient_update.astype(jnp.bfloat16)
    down_local = jnp.einsum(
        "rf,rk->fk", hid_act, gradient_update, preferred_element_type=jnp.float32
    )
    grad_act = jnp.einsum(
        "rk,fk->rf", gradient_update, down_cols, preferred_element_type=jnp.float32
    )
    grad_pre = (grad_act * gelu_slope(preact)).astype(jnp.bfloat16)
    up_local = jnp.einsum("rk,rf->kf", pnormed, grad_pre, preferred_element_type=jnp.float32)
    out_local = jnp.einsum(
        "rk,rd->kd", output_normalized, grad_pred, preferred_element_type=jnp.float32
    )
    grad_up, grad_out = tuple(
        (
            part.astype(jnp.float32)
            for part in sum_together(
                (up_local.astype(jnp.bfloat16), out_local.astype(jnp.bfloat16)), ROLE_DP, (0, 0)
            )
        )
    )
    grad_down = summed_on_arrival(down_local, ROLE_DP, 1)
    return (loss, grad_up, grad_down, grad_out)


def solution(mesh):
    finer = Mesh(
        mesh.devices.reshape(mesh.shape["role"], 4, 4, 4, 2),
        ("role", "dp_0", "dp_1", "mp_0", "mp_1"),
    )
    return jax.shard_map(
        body,
        mesh=finer,
        in_specs=(
            P(DP, MP),
            P(DP, None),
            P(ROLE_DP, MP),
            P(MP, ROLE_DP),
            P(ROLE_DP, MP),
            P(MP, ROLE_DP),
            P(ROLE_DP, MP),
            P(DP, None),
            P(DP),
            P(),
        ),
        out_specs=(P(), P(ROLE_DP, MP), P(MP, ROLE_DP), P(ROLE_DP, MP)),
        check_vma=False,
    )
```

profile of v0, /device:TPU:2, one launch (start us, length us, event | category | flops | bytes accessed | tf_op | source)
XLA Modules:
  0.0 619.0 jit_solution(12182839815354292576)
XLA Ops:
  9.5 1.4 broadcast_in_dim.10
  10.9 11.5 %all-to-all-start = ((bf16[32,192,12]{1,2,0:T(8,128)(2,1)}), bf16[32,192,12]{1,2,0:T(8,128)(2,1)S(1)}, u32[]{:S(2)}, u32[]{:S(2)}) async-start(bf16[32,192,12]{1,2,0:T(8,128)(2,1)} %broadcast_in_dim.10), calls=%async_computation | async-start | bytes 524288 | tf_op jit(solution)/shard_map/all_to_all | solution.py:30
  22.4 0.8 maximum_bitcast_fusion.1
  23.2 75.8 %all-gather.1 = bf16[32,12,352]{2,1,0:T(8,128)(2,1)S(1)} all-gather(bf16[1,12,352]{2,1,0:T(8,128)(2,1)S(1)} %maximum_bitcast_fusion.1), channel_id=1, replica_groups=mesh['role'=2,'dp_0'=4,'dp_1'=4,'mp_0'=4,'mp_1'=2] {'role','dp_0','dp_1'}, dimensions={0}, use_global_device_ids=true | all-gather | bytes 278784 | tf_op jit(solution)/shard_map/all_gather | solution.py:59
  99.8 0.9 reshape.189
  100.6 0.9 fusion.29
  101.6 1.3 broadcast_in_dim.11
  102.9 4.8 all-to-all-start.1
  107.7 1.6 fusion.61
  109.3 1.9 reshape.172
  111.2 2.6 fusion.79
  113.9 11.1 %all-to-all-done.1 = bf16[8,512,160]{1,2,0:T(8,128)(2,1)S(1)} async-done(((bf16[8,512,160]{1,2,0:T(8,128)(2,1)}), bf16[8,512,160]{1,2,0:T(8,128)(2,1)S(1)}, u32[]{:S(2)}, u32[]{:S(2)}) %all-to-all-start.1) | async-done | bytes 1310752 | tf_op jit(solution)/shard_map/all_to_all | solution.py:30
  124.9 32.0 %all-gather.6.cloned.1.call-done = bf16[1280,640]{1,0:T(8,128)(2,1)} async-done(((bf16[40,640]{1,0:T(8,128)(2,1)}), bf16[1280,640]{1,0:T(8,128)(2,1)}) %all-gather.6.cloned.1.call-update) | async-done | bytes 1638416 | tf_op jit(solution)/shard_map/all_gather | solution.py:153
  156.9 142.1 %all-gather.8.cloned.1.call-done = bf16[640,1280]{0,1:T(8,128)(2,1)} async-done(((bf16[640,40]{0,1:T(8,128)(2,1)}), bf16[640,1280]{0,1:T(8,128)(2,1)}) %all-gather.8.cloned.1.call-update) | async-done | bytes 1638416 | tf_op jit(solution)/shard_map/all_gather | solution.py:154
  299.0 8.5 %conditional.1 = (f32[512,1280]{1,0:T(8,128)}) conditional(s32[]{:T(128)} %convert_element_type.101, () %tuple.14, (bf16[512,8,160]{0,2,1:T(8,128)(2,1)S(1)}, bf16[1280,640]{1,0:T(8,128)(2,1)}, bf16[640,1280]{0,1:T(8,128)(2,1)}) %tuple.41), branch_computations={%region_5.0_spmd, %region_6.9_spmd} | conditional | flops 1687224832 | bytes 12470280 | solution.py:166
  299.7 1.4 fusion.1
  301.1 6.4 %fusion.10 = f32[512,1280]{1,0:T(8,128)} fusion(bf16[640,1280]{0,1:T(8,128)(2,1)} %get-tuple-element.25, bf16[512,1280]{0,1:T(8,128)(2,1)} %fusion.1, bf16[1280,640]{1,0:T(8,128)(2,1)} %get-tuple-element.11), kind=kOutput, calls=%fused_computation.14 | convolution fusion | flops 1680670720 | bytes 7208960 | tf_op jit(solution)/shard_map/cond/branch_1_fun/dot_general | solution.py:161
  307.5 3.2 copy.34
  312.0 5.7 all-to-all-start.3
  318.4 7.2 %all-to-all-done.3 = f32[16,1,1]{2,1,0:T(1,128)S(1)} async-done(((f32[16,1,1]{2,1,0:T(1,128)}), f32[16,1,1]{2,1,0:T(1,128)S(1)}, u32[]{:S(2)}, u32[]{:S(2)}) %all-to-all-start.3) | async-done | bytes 96 | tf_op jit(solution)/shard_map/all_to_all | solution.py:30
  326.9 1.8 fusion.81
  329.3 13.2 %reduce-scatter.3.cloned.1.call-done = f32[512,160]{0,1:T(8,128)} async-done(((f32[512,1280]{0,1:T(8,128)}), f32[512,160]{0,1:T(8,128)}) %reduce-scatter.3.cloned.1.call-update) | async-done | bytes 327696 | tf_op jit(solution)/shard_map/reduce_scatter | solution.py:167
  342.5 1.1 fusion.67
  344.2 7.0 %all-to-all-start.2 = ((f32[8,1,1024]{2,1,0:T(1,128)}), f32[8,1,1024]{2,1,0:T(1,128)S(1)}, u32[]{:S(2)}, u32[]{:S(2)}) async-start(f32[8,1,1024]{2,1,0:T(1,128)} %broadcast_in_dim.12), calls=%async_computation.3 | async-start | bytes 65536 | tf_op jit(solution)/shard_map/all_to_all | solution.py:30
  351.2 4.0 all-to-all-done.2
  355.3 1.0 multiply_convert_fusion.2
  356.3 7.8 %collective-permute-start = (bf16[512,160]{0,1:T(8,128)(2,1)S(1)}, bf16[512,160]{0,1:T(8,128)(2,1)S(1)}, u32[]{:S(2)}, u32[]{:S(2)}) collective-permute-start(bf16[512,160]{0,1:T(8,128)(2,1)S(1)} %multiply_convert_fusion.2), channel_id=1, source_target_pairs={{0,128},{1,129},{2,130},{3,131},{4,132},{5,133},{6,134},{7,135},{8... | collective-permute-start | bytes 491528 | tf_op jit(solution)/shard_map/ppermute | solution.py:53
  364.5 3.0 collective-permute-done
  367.5 1.5 multiply_convert_fusion.1
  369.0 1.7 fusion.63
  371.0 36.0 %reduce-scatter.5.cloned.1.call-done = f32[128,384]{1,0:T(8,128)} async-done(((f32[1024,384]{1,0:T(8,128)}), f32[128,384]{1,0:T(8,128)}) %reduce-scatter.5.cloned.1.call-update) | async-done | bytes 196624 | tf_op jit(solution)/shard_map/reduce_scatter | solution.py:74
  407.0 1.5 convolution_convert_fusion
  408.8 27.1 %all-gather.10.cloned.1.call-done = f32[1024,384]{1,0:T(8,128)} async-done(((f32[128,384]{1,0:T(8,128)}), f32[1024,384]{1,0:T(8,128)}) %all-gather.10.cloned.1.call-update) | async-done | bytes 1572880 | tf_op jit(solution)/shard_map/all_gather | solution.py:77
  436.0 2.2 multiply_reduce_fusion.1
  438.2 0.9 multiply_convert_fusion
  439.2 0.9 copy-done.12
  441.2 2.3 fusion.30
  443.5 0.8 reshape.177
  444.4 10.0 %all-to-all-start.4 = ((f32[32,192,12]{1,2,0:T(8,128)}), f32[32,192,12]{1,2,0:T(8,128)S(1)}, u32[]{:S(2)}, u32[]{:S(2)}) async-start(f32[32,192,12]{1,2,0:T(8,128)} %bitcast.9), calls=%async_computation.6 | async-start | bytes 1048576 | tf_op jit(solution)/shard_map/all_to_all | solution.py:102
  454.8 0.9 reshape.176
  456.4 16.2 %psum.43 = f32[]{:T(128)} all-reduce(f32[]{:T(128)S(6)} %mul.192), channel_id=1, replica_groups=mesh['role'=2,'dp_0'=4,'dp_1'=4,'mp_0'=4,'mp_1'=2] {'role'}, use_global_device_ids=true, to_apply=%region_14.0 | all-reduce | flops 1 | bytes 8 | tf_op jit(solution)/shard_map/psum | solution.py:64
  472.6 10.4 %psum.44 = f32[]{:T(128)} all-reduce(f32[]{:T(128)} %psum.43), channel_id=1, replica_groups=mesh['role'=2,'dp_0'=4,'dp_1'=4,'mp_0'=4,'mp_1'=2] {'dp_0'}, use_global_device_ids=true, to_apply=%region_15.0 | all-reduce | flops 1 | bytes 8 | tf_op jit(solution)/shard_map/psum | solution.py:64
  483.6 10.3 %psum.45 = f32[]{:T(128)} all-reduce(f32[]{:T(128)} %psum.44), channel_id=1, replica_groups=mesh['role'=2,'dp_0'=4,'dp_1'=4,'mp_0'=4,'mp_1'=2] {'dp_1'}, use_global_device_ids=true, to_apply=%region_16.0 | all-reduce | flops 1 | bytes 8 | tf_op jit(solution)/shard_map/psum | solution.py:64
  494.5 10.4 %psum.46 = f32[]{:T(128)} all-reduce(f32[]{:T(128)} %psum.45), channel_id=1, replica_groups=mesh['role'=2,'dp_0'=4,'dp_1'=4,'mp_0'=4,'mp_1'=2] {'mp_0'}, use_global_device_ids=true, to_apply=%region_17.0 | all-reduce | flops 1 | bytes 8 | tf_op jit(solution)/shard_map/psum | solution.py:64
  504.9 3.1 psum.47
  508.6 98.4 %all-reduce.7.cloned.1.call-done = bf16[1280,128]{1,0:T(8,128)(2,1)} async-done(((bf16[1280,128]{1,0:T(8,128)(2,1)}), bf16[1280,128]{1,0:T(8,128)(2,1)}) %all-reduce.7.cloned.1.call-update) | async-done | bytes 327696
  607.1 0.7 dynamic-slice_convert_fusion
  608.4 0.7 dynamic-slice_convert_fusion.1
  (80 shorter events, 10.7 us)
Async XLA Ops:
  8.0 92.6 %copy-start = (bf16[1568,160]{0,1:T(8,128)(2,1)S(1)}, bf16[1568,160]{0,1:T(8,128)(2,1)}, u32[]{:S(2)}) copy-start(bf16[1568,160]{0,1:T(8,128)(2,1)} %param.12) | copy-start | bytes 1505284
  8.0 91.0 %copy-start.1 = (bf16[1024,384]{1,0:T(8,128)(2,1)S(1)}, bf16[1024,384]{1,0:T(8,128)(2,1)}, u32[]{:S(2)}) copy-start(bf16[1024,384]{1,0:T(8,128)(2,1)} %param.13) | copy-start | bytes 2359300
  8.0 91.7 %copy-start.14 = (s32[1,1024]{1,0:T(1,128)S(1)}, s32[1,1024]{1,0:T(1,128)}, u32[]{:S(2)}) copy-start(s32[1,1024]{1,0:T(1,128)} %param.19) | copy-start | bytes 12292
  8.0 148.9 %all-gather.6.cloned.1.call-start = ((), (), s32[]{:S(2)}) async-start(), calls=%async_computation.8 | async-start | bytes 1689600 | tf_op jit(solution)/shard_map/all_gather | solution.py:153
  8.8 290.2 %all-gather.8.cloned.1.call-start = ((), (), s32[]{:S(2)}) async-start(), calls=%async_computation.9 | async-start | bytes 1689600 | tf_op jit(solution)/shard_map/all_gather | solution.py:154
  10.9 90.7 %all-to-all-start = ((bf16[32,192,12]{1,2,0:T(8,128)(2,1)}), bf16[32,192,12]{1,2,0:T(8,128)(2,1)S(1)}, u32[]{:S(2)}, u32[]{:S(2)}) async-start(bf16[32,192,12]{1,2,0:T(8,128)(2,1)} %broadcast_in_dim.10), calls=%async_computation | async-start | bytes 524288 | tf_op jit(solution)/shard_map/all_to_all | solution.py:30
  101.6 1.3 copy-start.9
  101.6 1.3 copy-start.11
  102.9 22.0 %all-to-all-start.1 = ((bf16[8,512,160]{1,2,0:T(8,128)(2,1)}), bf16[8,512,160]{1,2,0:T(8,128)(2,1)S(1)}, u32[]{:S(2)}, u32[]{:S(2)}) async-start(bf16[8,512,160]{1,2,0:T(8,128)(2,1)} %broadcast_in_dim.11), calls=%async_computation.1 | async-start | bytes 2621440 | tf_op jit(solution)/shard_map/all_to_all | solution.py:30
  107.7 219.2 %all-reduce.5.cloned.1.call-start = ((), (), s32[]{:S(2)}) async-start(), calls=%async_computation.7 | async-start | bytes 3145728 | tf_op jit(solution)/shard_map/psum | solution.py:197
  109.3 4.5 copy-start.4
  113.8 228.6 %reduce-scatter.3.cloned.1.call-start = ((), (), s32[]{:S(2)}) async-start(), calls=%async_computation.10 | async-start | bytes 2949120 | tf_op jit(solution)/shard_map/reduce_scatter | solution.py:167
  312.0 13.6 %all-to-all-start.3 = ((f32[16,1,1]{2,1,0:T(1,128)}), f32[16,1,1]{2,1,0:T(1,128)S(1)}, u32[]{:S(2)}, u32[]{:S(2)}) async-start(f32[16,1,1]{2,1,0:T(1,128)} %broadcast_in_dim.13), calls=%async_computation.4 | async-start | bytes 16384 | tf_op jit(solution)/shard_map/all_to_all | solution.py:30
  326.8 1.9 copy-start.2
  328.7 13.8 %copy-start.10 = (bf16[512,160]{0,1:T(8,128)(2,1)S(1)}, bf16[512,160]{0,1:T(8,128)(2,1)}, u32[]{:S(2)}) copy-start(bf16[512,160]{0,1:T(8,128)(2,1)} %copy-done.9) | copy-start | bytes 491524
  344.2 11.1 %all-to-all-start.2 = ((f32[8,1,1024]{2,1,0:T(1,128)}), f32[8,1,1024]{2,1,0:T(1,128)S(1)}, u32[]{:S(2)}, u32[]{:S(2)}) async-start(f32[8,1,1024]{2,1,0:T(1,128)} %broadcast_in_dim.12), calls=%async_computation.3 | async-start | bytes 65536 | tf_op jit(solution)/shard_map/all_to_all | solution.py:30
  351.2 55.7 %reduce-scatter.5.cloned.1.call-start = ((), (), s32[]{:S(2)}) async-start(), calls=%async_computation.11 | async-start | bytes 1769472 | tf_op jit(solution)/shard_map/reduce_scatter | solution.py:74
  356.3 11.2 %copy-start.8 = (bf16[384,352]{1,0:T(8,128)(2,1)S(1)}, bf16[384,352]{1,0:T(8,128)(2,1)}, u32[]{:S(2)}) copy-start(bf16[384,352]{1,0:T(8,128)(2,1)} %reshape.189) | copy-start | bytes 811012
  356.3 11.1 %collective-permute-start = (bf16[512,160]{0,1:T(8,128)(2,1)S(1)}, bf16[512,160]{0,1:T(8,128)(2,1)S(1)}, u32[]{:S(2)}, u32[]{:S(2)}) collective-permute-start(bf16[512,160]{0,1:T(8,128)(2,1)S(1)} %multiply_convert_fusion.2), channel_id=1, source_target_pairs={{0,128},{1,129},{2,130},{3,131},{4,132},{5,133},{6,134},{7,135},{8... | collective-permute-start | bytes 491528 | tf_op jit(solution)/shard_map/ppermute | solution.py:53
  364.5 4.5 copy-start.7
  370.7 65.2 %all-gather.10.cloned.1.call-start = ((), (), s32[]{:S(2)}) async-start(), calls=%async_computation.12 | async-start | bytes 1769472 | tf_op jit(solution)/shard_map/all_gather | solution.py:77
  436.0 2.3 copy-start.3
  438.2 1.8 copy-start.5
  439.2 0.9 copy-start.12
  440.1 1.1 copy-start.6
  440.1 1.2 copy-start.13
  444.4 38.6 %copy-start.15 = (u32[256]{0:T(256)S(1)}, u32[256]{0:T(256)}, u32[]{:S(2)}) copy-start(u32[256]{0:T(256)} %constant.79) | copy-start | bytes 3076
  444.4 165.4 %all-to-all-start.4 = ((f32[32,192,12]{1,2,0:T(8,128)}), f32[32,192,12]{1,2,0:T(8,128)S(1)}, u32[]{:S(2)}, u32[]{:S(2)}) async-start(f32[32,192,12]{1,2,0:T(8,128)} %bitcast.9), calls=%async_computation.6 | async-start | bytes 1048576 | tf_op jit(solution)/shard_map/all_to_all | solution.py:102
  454.4 152.7 %all-reduce.7.cloned.1.call-start = ((), (), s32[]{:S(2)}) async-start(), calls=%async_computation.13 | async-start | bytes 655360
Sparse Core Ops, SparseCore 0:
  10.6 146.2 all-gather.5
  158.7 140.2 all-gather.7
  458.6 148.3 all-reduce.6
Sparse Core Ops, SparseCore 1:
  113.9 67.6 all-reduce.4
  310.8 31.6 reduce-scatter.2
  370.8 36.1 reduce-scatter.4
  408.8 27.1 all-gather.9
where the time goes:
time: 620 us; the launch traced here: 619 us
  waiting for transfers between devices  375 us (60%)
  blocking collectives  126 us (20%)
  starting transfers between devices  47.1 us (8%)
  between operations  20.9 us (3%)
  matrix products  19.1 us (3%)
  local copies, waits for them, and re-layouts  15.9 us (3%)
  other arithmetic  14.2 us (2%)
    all_gather x1, waiting for transfers between devices, body(): down_rows = lax.all_gather(ema_down, ROLE_DP, axis=1, tiled=True)  142 us
    unnamed x8, waiting for transfers between devices  99.9 us
    all_gather x1, blocking collectives, sent_together(): filled = lax.all_gather(both, axis, axis=dim, tiled=True)  75.8 us
    psum x5, blocking collectives, by_axis(): return functools.reduce(lax.psum, axes, shard)  50.4 us
    reduce_scatter x1, waiting for transfers between devices, sum_by_parts(): lax.psum_scatter(filled_up(lines, lax.axis_size(axis)), axis, scatter_dim...  36 us
    all_gather x1, waiting for transfers between devices, body(): up_cols = lax.all_gather(ema_up, ROLE_DP, axis=0, tiled=True)  32 us
    all_to_all x4, starting transfers between devices, from_everyone(): return lax.all_to_all(copies, axis, split_axis=0, concat_axis=0, tiled=True)  29 us
    all_gather x1, waiting for transfers between devices, sum_by_parts(): whole = lax.all_gather(own, axis).reshape(-1, *lines.shape[1:])  27.1 us
  transfers between devices with their start and end apart: 13, of which 10 were waited for; matrix products, arithmetic and copies ran while one was open for 6% of the time, Pallas kernels for 0%

commit v1 on v0

v1 whole, which is shorter than its diff:
```python
import jax
import jax.numpy as jnp
from jax import lax
from jax.sharding import Mesh
from jax.sharding import PartitionSpec as P

D = 1280
PW = 384
TOK = 1568
MMAX = 1024
X = "mp_0"
CORE = "mp_1"
Y = "dp_0"
Z = ("role", "dp_1")
MP = ("mp_0", "mp_1")
DP = ("dp_0", "dp_1")
ROLE_DP = ("role", "dp_0", "dp_1")

HALF = MMAX // 2
QUARTER = HALF // 2
OWN = QUARTER // 4
EPS = 1e-06
COEF = 0.7978845608028654
BF16 = jnp.bfloat16
F32 = jnp.float32


def spread(block, axis):
    copies = jnp.broadcast_to(block, (lax.axis_size(axis), *block.shape))
    return lax.all_to_all(copies, axis, split_axis=0, concat_axis=0, tiled=True)


def exchanged(pieces, axis):
    return lax.all_to_all(pieces, axis, split_axis=0, concat_axis=0, tiled=True)


def swapped(block):
    return lax.ppermute(block, CORE, [(0, 1), (1, 0)])


def normalize(values, axis=-1):
    row_mean = jnp.mean(values, axis=axis, keepdims=True)
    row_deviations = values - row_mean
    variance = jnp.mean(row_deviations * row_deviations, axis=axis, keepdims=True)
    return row_deviations * lax.rsqrt(variance + EPS)


def gelu_slope(values):
    inner = COEF * (values + 0.044715 * values * values * values)
    tangent = jnp.tanh(inner)
    return 0.5 * (1.0 + tangent) + 0.5 * values * (1.0 - tangent * tangent) * COEF * (
        1.0 + 3.0 * 0.044715 * values * values
    )


def two_parts(value):
    high = lax.reduce_precision(value, 8, 7)
    return jnp.stack([high, lax.reduce_precision(value - high, 8, 7)]).astype(BF16)


def core_major(gathered):
    width = gathered.shape[-1]
    blocks = gathered.reshape(2, 2, 2, 4, -1, width)
    return blocks.transpose(1, 2, 0, 3, 4, 5).reshape(D, width)


def body(
    patches,
    pred_states,
    ema_up,
    ema_down,
    pred_up,
    pred_down,
    pred_out,
    masked_index,
    masked_count,
    loss_scale,
):
    role = lax.axis_index("role")
    core = lax.axis_index(CORE)
    first = core == 0
    start = role * HALF
    own_start = start + core * QUARTER
    other_start = start + (1 - core) * QUARTER
    tile_start = own_start + lax.axis_index(X) * OWN

    both = jnp.concatenate([ema_up, ema_down.T], axis=0)
    along_z = spread(both, Z).reshape(-1, both.shape[1])
    along_y = spread(along_z, Y).reshape(4, 8, 2, 40, both.shape[1])
    up_cols = core_major(along_y[:, :, 0])
    down_rows = core_major(along_y[:, :, 1])

    count = (masked_count[0] // 8).astype(BF16)
    tail = jnp.full((pred_up.shape[0], 96), count, BF16)
    small = jnp.concatenate([pred_up, pred_down.T, pred_out, tail], axis=1)
    small = spread(small, ROLE_DP)
    total = 8.0 * jnp.sum(small[:16, 0, 544].astype(F32))
    small = small.reshape(PW, -1)
    up_rows = small[:, :192]
    down_cols = small[:, 192:384]
    out_x = spread(small[:, 384:544], X)
    out_x = out_x.transpose(1, 0, 2).reshape(PW, D // 2)
    out_other = swapped(out_x)
    out_full = jnp.where(
        first,
        jnp.concatenate([out_x, out_other], axis=1),
        jnp.concatenate([out_other, out_x], axis=1),
    )

    index = jnp.concatenate(
        [
            lax.dynamic_slice_in_dim(masked_index[0], own_start, QUARTER),
            lax.dynamic_slice_in_dim(masked_index[0], other_start, QUARTER),
        ]
    )
    onehot = (jnp.arange(TOK, dtype=jnp.int32)[:, None] == index[None, :]).astype(BF16)
    picked = jnp.einsum("tw,tk->wk", patches, onehot, preferred_element_type=F32).astype(BF16)
    mine = spread(picked, X).reshape(D // 2, HALF)
    theirs = swapped(mine)
    theirs = jnp.concatenate([theirs[:, QUARTER:], theirs[:, :QUARTER]], axis=1)
    whole = jnp.concatenate(
        [jnp.where(first, mine, theirs), jnp.where(first, theirs, mine)], axis=0
    )
    normed = normalize(whole.astype(F32), 0).astype(BF16)
    hidden = jax.nn.gelu(
        jnp.einsum("dr,dh->rh", normed, up_cols, preferred_element_type=F32), approximate=True
    ).astype(BF16)
    for_other = jnp.einsum("rh,dh->rd", hidden[QUARTER:], down_rows, preferred_element_type=F32)
    for_own = jnp.einsum("rh,dh->rd", hidden[:QUARTER], down_rows, preferred_element_type=F32)
    chip_sum = (for_own + swapped(for_other)).astype(BF16)
    arrived = exchanged(chip_sum.reshape(4, OWN, D), X)
    residual = lax.dynamic_slice_in_dim(whole, lax.axis_index(X) * OWN, OWN, 1).T
    block_out = residual.astype(F32) + jnp.sum(arrived.astype(F32), axis=0)
    targets = normalize(block_out).astype(BF16)

    states = jnp.concatenate(
        [
            lax.dynamic_slice_in_dim(pred_states, own_start, QUARTER),
            lax.dynamic_slice_in_dim(pred_states, other_start, QUARTER),
        ]
    ).astype(F32)
    pnormed = normalize(states).astype(BF16)
    preact = jnp.dot(pnormed, up_rows, preferred_element_type=F32)
    hid_act = jax.nn.gelu(preact, approximate=True).astype(BF16)
    mix = jnp.einsum("rf,kf->rk", hid_act, down_cols, preferred_element_type=F32)
    mix = mix[:QUARTER] + swapped(mix[QUARTER:])
    mix = jnp.sum(exchanged(mix.reshape(4, OWN, PW), X), axis=0)
    updated = lax.dynamic_slice_in_dim(pred_states, tile_start, OWN).astype(F32) + mix
    deviations = updated - jnp.mean(updated, axis=-1, keepdims=True)
    reciprocal_spread = lax.rsqrt(jnp.mean(deviations * deviations, axis=-1, keepdims=True) + EPS)
    standardized = deviations * reciprocal_spread
    outnorm = standardized.astype(BF16)
    predicted = jnp.dot(outnorm, out_full, preferred_element_type=F32)
    slots = tile_start + jnp.arange(OWN, dtype=jnp.int32)
    live = (slots < masked_count[0]).astype(F32)[:, None]
    norm_scale = total * float(D)
    residue = predicted - targets.astype(F32)
    smooth = jnp.sqrt(residue * residue + 1.0)
    local_loss = jnp.sum(live * (smooth - 1.0))
    grad_pred = (loss_scale * live * residue / smooth / norm_scale).astype(BF16)
    grad_norm = jnp.einsum("rd,kd->rk", grad_pred, out_full, preferred_element_type=F32)
    grad_upd = reciprocal_spread * (
        grad_norm
        - jnp.mean(grad_norm, axis=-1, keepdims=True)
        - standardized * jnp.mean(grad_norm * standardized, axis=-1, keepdims=True)
    )

    loss_lines = jnp.zeros((16, PW), BF16).at[0, :2].set(two_parts(local_loss))
    lines = jnp.concatenate([grad_upd.astype(BF16), loss_lines], axis=0)
    own_lines = spread(lines, X)
    other_lines = swapped(own_lines)
    rows = jnp.concatenate(
        [own_lines[:, :OWN].reshape(QUARTER, PW), other_lines[:, :OWN].reshape(QUARTER, PW)]
    )
    group_loss = jnp.sum(own_lines[:, OWN, :2].astype(F32)) + jnp.sum(
        other_lines[:, OWN, :2].astype(F32)
    )

    near = jnp.where(first, grad_pred[:, : D // 2], grad_pred[:, D // 2 :])
    far = jnp.where(first, grad_pred[:, D // 2 :], grad_pred[:, : D // 2])
    out_far = jnp.einsum("rk,rd->kd", outnorm, far, preferred_element_type=F32)
    out_near = jnp.einsum("rk,rd->kd", outnorm, near, preferred_element_type=F32)
    out_chip = (out_near + swapped(out_far)).astype(BF16)
    out_local = exchanged(out_chip.reshape(PW, 4, 160).transpose(1, 0, 2), X)
    out_local = jnp.sum(out_local.astype(F32), axis=0).astype(BF16)
    down_local = jnp.einsum("rk,rf->kf", rows, hid_act, preferred_element_type=F32)
    grad_act = jnp.einsum("rk,kf->rf", rows, down_cols, preferred_element_type=F32)
    grad_pre = (grad_act * gelu_slope(preact)).astype(BF16)
    up_local = jnp.einsum("rk,rf->kf", pnormed, grad_pre, preferred_element_type=F32)
    end = jnp.broadcast_to(jnp.pad(two_parts(group_loss), (0, 94)), (PW, 96))
    sent = jnp.concatenate(
        [up_local.astype(BF16), down_local.astype(BF16), out_local, end], axis=1
    )
    sums = exchanged(sent.reshape(32, PW // 32, -1), ROLE_DP)
    sums = jnp.sum(sums.astype(F32), axis=0)
    grad_up = sums[:, :192]
    grad_down = sums[:, 192:384].T
    grad_out = sums[:, 384:544]
    loss = jnp.sum(sums[0, 544:546]) / norm_scale
    return (loss, grad_up, grad_down, grad_out)


def solution(mesh):
    finer = Mesh(
        mesh.devices.reshape(mesh.shape["role"], 4, 4, 4, 2),
        ("role", "dp_0", "dp_1", "mp_0", "mp_1"),
    )
    return jax.shard_map(
        body,
        mesh=finer,
        in_specs=(
            P(DP, MP),
            P(DP, None),
            P(ROLE_DP, MP),
            P(MP, ROLE_DP),
            P(ROLE_DP, MP),
            P(MP, ROLE_DP),
            P(ROLE_DP, MP),
            P(DP, None),
            P(DP),
            P(),
        ),
        out_specs=(P(), P(ROLE_DP, MP), P(MP, ROLE_DP), P(ROLE_DP, MP)),
        check_vma=False,
    )
```

time: 620 us -> 249 us (0.40)
  waiting for transfers between devices: 375 us -> 102 us
  blocking collectives: 126 us -> 34.3 us
  between operations: 20.9 us -> 12.2 us
    all_gather x3 -> x0, waiting for transfers between devices: 201 us -> none  [the longest x1 142 us: body(): down_rows = lax.all_gather(ema_down, ROLE_DP, axis=1, tiled=True)]
    unnamed x8 -> x0, waiting for transfers between devices: 99.9 us -> none
    all_to_all x5 -> x8, waiting for transfers between devices: 22.2 us -> 101 us  [the longest x5 84.9 us: spread(): return lax.all_to_all(copies, axis, split_axis=0, concat_axis=0, tiled=True)]
    all_gather x1 -> x0, blocking collectives: 75.8 us -> none  [sent_together(): filled = lax.all_gather(both, axis, axis=dim, tiled=True)]
    psum x5 -> x0, blocking collectives: 50.4 us -> none  [by_axis(): return functools.reduce(lax.psum, axes, shard)]
    reduce_scatter x2 -> x0, waiting for transfers between devices: 49.2 us -> none  [the longest x1 36 us: sum_by_parts(): lax.psum_scatter(filled_up(lines, lax.axis_size(axis)), axis, scatter_dim...]
    all_to_all x0 -> x2, blocking collectives: none -> 34.3 us  [the longest x1 24.4 us: exchanged(): return lax.all_to_all(pieces, axis, split_axis=0, concat_axis=0, tiled=True)]
    all_to_all x5 -> x8, starting transfers between devices: 39 us -> 46.4 us  [the longest x5 31.1 us: spread(): return lax.all_to_all(copies, axis, split_axis=0, concat_axis=0, tiled=True)]
  transfers between devices with their start and end apart: 13 -> 14, of which waited for: 10 -> 9; matrix products, arithmetic and copies ran while one was open for 6% -> 14% of each run, Pallas kernels for 0% -> 0%
where the time goes in v1:
time: 249 us; the launch traced here: 247 us
  waiting for transfers between devices  102 us (41%)
  starting transfers between devices  47.1 us (19%)
  blocking collectives  34.3 us (14%)
  local copies, waits for them, and re-layouts  19.8 us (8%)
  matrix products  16.8 us (7%)
  other arithmetic  15 us (6%)
  between operations  12.2 us (5%)
    all_to_all x5, waiting for transfers between devices, spread(): return lax.all_to_all(copies, axis, split_axis=0, concat_axis=0, tiled=True)  84.9 us
    all_to_all x5, starting transfers between devices, spread(): return lax.all_to_all(copies, axis, split_axis=0, concat_axis=0, tiled=True)  31.1 us
    all_to_all x1, blocking collectives, exchanged(): return lax.all_to_all(pieces, axis, split_axis=0, concat_axis=0, tiled=True)  24.4 us
    all_to_all x3, waiting for transfers between devices, exchanged(): return lax.all_to_all(pieces, axis, split_axis=0, concat_axis=0, tiled=True)  16.4 us
    all_to_all x3, starting transfers between devices, exchanged(): return lax.all_to_all(pieces, axis, split_axis=0, concat_axis=0, tiled=True)  15.3 us
    all_to_all x1, blocking collectives, spread(): return lax.all_to_all(copies, axis, split_axis=0, concat_axis=0, tiled=True)  9.83 us
    broadcast_in_dim x6, local copies, waits for them, and re-layouts, spread(): copies = jnp.broadcast_to(block, (lax.axis_size(axis), *block.shape))  6.5 us
  transfers between devices with their start and end apart: 14, of which 9 were waited for; matrix products, arithmetic and copies ran while one was open for 14% of the time, Pallas kernels for 0%

profile of v1, /device:TPU:2, one launch (start us, length us, event | category | flops | bytes accessed | tf_op | source)
XLA Modules:
  0.0 247.2 jit_solution(12366960493991524258)
XLA Ops:
  0.7 0.8 constant_dynamic-slice_fusion.1
  2.4 0.9 broadcast_in_dim.19
  3.3 5.8 %all-to-all-start.3 = ((bf16[4,160,512]{2,1,0:T(8,128)(2,1)}), bf16[4,160,512]{2,1,0:T(8,128)(2,1)S(1)}, u32[]{:S(2)}, u32[]{:S(2)}) async-start(bf16[4,160,512]{2,1,0:T(8,128)(2,1)} %broadcast_in_dim.19), calls=%async_computation.3 | async-start | bytes 1310720 | tf_op jit(solution)/shard_map/all_to_all | solution.py:30
  10.0 7.7 %all-to-all-done.3 = bf16[4,160,512]{2,1,0:T(8,128)(2,1)S(1)} async-done(((bf16[4,160,512]{2,1,0:T(8,128)(2,1)}), bf16[4,160,512]{2,1,0:T(8,128)(2,1)S(1)}, u32[]{:S(2)}, u32[]{:S(2)}) %all-to-all-start.3) | async-done | bytes 655392 | tf_op jit(solution)/shard_map/all_to_all | solution.py:30
  17.7 0.9 broadcast_in_dim.17
  18.6 11.5 %all-to-all-start = ((bf16[32,12,640]{2,1,0:T(8,128)(2,1)}), bf16[32,12,640]{2,1,0:T(8,128)(2,1)S(1)}, u32[]{:S(2)}, u32[]{:S(2)}) async-start(bf16[32,12,640]{2,1,0:T(8,128)(2,1)} %broadcast_in_dim.17), calls=%async_computation | async-start | bytes 1310720 | tf_op jit(solution)/shard_map/all_to_all | solution.py:30
  30.1 20.1 %all-to-all-done = bf16[32,12,640]{2,1,0:T(8,128)(2,1)S(1)} async-done(((bf16[32,12,640]{2,1,0:T(8,128)(2,1)}), bf16[32,12,640]{2,1,0:T(8,128)(2,1)S(1)}, u32[]{:S(2)}, u32[]{:S(2)}) %all-to-all-start) | async-done | bytes 491552 | tf_op jit(solution)/shard_map/all_to_all | solution.py:30
  50.2 1.0 broadcast_in_dim.20
  51.2 3.5 %all-to-all-start.4 = ((bf16[8,80,640]{2,1,0:T(8,128)(2,1)}), bf16[8,80,640]{2,1,0:T(8,128)(2,1)S(1)}, u32[]{:S(2)}, u32[]{:S(2)}) async-start(bf16[8,80,640]{2,1,0:T(8,128)(2,1)} %broadcast_in_dim.20), calls=%async_computation.4 | async-start | bytes 1638400 | tf_op jit(solution)/shard_map/all_to_all | solution.py:30
  54.8 21.3 %all-to-all-done.4 = bf16[8,80,640]{2,1,0:T(8,128)(2,1)S(1)} async-done(((bf16[8,80,640]{2,1,0:T(8,128)(2,1)}), bf16[8,80,640]{2,1,0:T(8,128)(2,1)S(1)}, u32[]{:S(2)}, u32[]{:S(2)}) %all-to-all-start.4) | async-done | bytes 819232 | tf_op jit(solution)/shard_map/all_to_all | solution.py:30
  76.1 2.0 broadcast_in_dim.21
  78.1 4.7 %all-to-all-start.5 = ((bf16[4,640,640]{2,1,0:T(8,128)(2,1)}), bf16[4,640,640]{2,1,0:T(8,128)(2,1)}, u32[]{:S(2)}, u32[]{:S(2)}) async-start(bf16[4,640,640]{2,1,0:T(8,128)(2,1)} %broadcast_in_dim.21), calls=%async_computation.5 | async-start | bytes 6553600 | tf_op jit(solution)/shard_map/all_to_all | solution.py:30
  82.8 1.1 constant_dynamic-slice_fusion.3
  85.4 1.2 fusion.54
  87.0 0.9 copy-done.1
  87.9 0.8 slice.109
  90.3 29.0 %all-to-all-done.5 = bf16[4,640,640]{2,1,0:T(8,128)(2,1)} async-done(((bf16[4,640,640]{2,1,0:T(8,128)(2,1)}), bf16[4,640,640]{2,1,0:T(8,128)(2,1)}, u32[]{:S(2)}, u32[]{:S(2)}) %all-to-all-start.5) | async-done | bytes 3276832 | tf_op jit(solution)/shard_map/all_to_all | solution.py:30
  119.3 2.2 fusion.103
  121.9 1.4 fusion.14
  123.3 1.8 fusion.51
  125.1 1.6 slice.110
  126.7 1.7 copy.65
  128.4 1.7 broadcast_in_dim.18
  130.1 5.5 %all-to-all-start.2 = ((bf16[4,384,160]{1,2,0:T(8,128)(2,1)}), bf16[4,384,160]{1,2,0:T(8,128)(2,1)}, u32[]{:S(2)}, u32[]{:S(2)}) async-start(bf16[4,384,160]{1,2,0:T(8,128)(2,1)} %broadcast_in_dim.18), calls=%async_computation.2 | async-start | bytes 983040 | tf_op jit(solution)/shard_map/all_to_all | solution.py:30
  135.7 1.9 slice_add_fusion
  137.6 6.8 %all-to-all-done.2 = bf16[4,384,160]{1,2,0:T(8,128)(2,1)} async-done(((bf16[4,384,160]{1,2,0:T(8,128)(2,1)}), bf16[4,384,160]{1,2,0:T(8,128)(2,1)}, u32[]{:S(2)}, u32[]{:S(2)}) %all-to-all-start.2) | async-done | bytes 491552 | tf_op jit(solution)/shard_map/all_to_all | solution.py:30
  144.4 5.5 %all-to-all-start.1 = ((f32[4,64,384]{2,1,0:T(8,128)}), f32[4,64,384]{2,1,0:T(8,128)}, u32[]{:S(2)}, u32[]{:S(2)}) async-start(f32[4,64,384]{2,1,0:T(8,128)} %bitcast.59), calls=%async_computation.1 | async-start | bytes 786432 | tf_op jit(solution)/shard_map/all_to_all | solution.py:34
  150.6 1.5 fusion.83
  152.8 3.9 %all-to-all-done.1 = f32[4,64,384]{2,1,0:T(8,128)} async-done(((f32[4,64,384]{2,1,0:T(8,128)}), f32[4,64,384]{2,1,0:T(8,128)}, u32[]{:S(2)}, u32[]{:S(2)}) %all-to-all-start.1) | async-done | bytes 393248 | tf_op jit(solution)/shard_map/all_to_all | solution.py:34
  156.7 1.7 reduce_sum.176
  158.4 1.6 fusion.102
  160.0 3.0 %fusion.5 = bf16[256,1280]{1,0:T(8,128)(2,1)} fusion(f32[256,1280]{1,0:T(8,128)} %collective-permute-done.3, bf16[1280,640]{1,0:T(8,128)(2,1)S(1)} %bitcast.52, bf16[512,640]{1,0:T(8,128)(2,1)} %copy-done.9), kind=kOutput, calls=%fused_computation.9 | convolution fusion | flops 420085760 | bytes 3932160 | tf_op jit(solution)/shard_map/rh,dh->rd/dot_general | solution.py:129
  163.1 4.9 %all-to-all-start.6 = ((bf16[4,64,1280]{2,1,0:T(8,128)(2,1)}), bf16[4,64,1280]{2,1,0:T(8,128)(2,1)S(1)}, u32[]{:S(2)}, u32[]{:S(2)}) async-start(bf16[4,64,1280]{2,1,0:T(8,128)(2,1)} %bitcast.57), calls=%async_computation.6 | async-start | bytes 1310720 | tf_op jit(solution)/shard_map/all_to_all | solution.py:34
  168.0 1.1 multiply_reduce_fusion.3
  169.1 1.0 fusion.72
  170.1 6.3 %all-to-all-done.6 = bf16[4,64,1280]{2,1,0:T(8,128)(2,1)S(1)} async-done(((bf16[4,64,1280]{2,1,0:T(8,128)(2,1)}), bf16[4,64,1280]{2,1,0:T(8,128)(2,1)S(1)}, u32[]{:S(2)}, u32[]{:S(2)}) %all-to-all-start.6) | async-done | bytes 655392 | tf_op jit(solution)/shard_map/all_to_all | solution.py:34
  176.8 2.7 %multiply_reduce_fusion = (f32[]{:T(128)}, bf16[64,1280]{1,0:T(8,128)(2,1)S(1)}) fusion(f32[64]{0:T(128)S(1)} %compare_convert_fusion, f32[]{:T(128)S(6)} %mul.211, f32[64]{0:T(128)S(1)} %get-tuple-element.37, f32[64]{0:T(128)S(1)} %get-tuple-element.38, f32[64,1280]{1,0:T(8,128)S(1)} %get-tuple-element.19, f32[64]{0:T(128)S(1)} %broadcast_multiply_fusion.2, ...), kind=kOutput, calls=%fused_computation.78 | convolution fusion | flops 68485120 | bytes 1524745 | tf_op jit(solution)/shard_map/dot_general | solution.py:153
  182.9 2.0 fusion.100
  185.4 0.7 fusion.82
  186.3 9.8 %all_to_all.50 = bf16[4,80,384]{2,1,0:T(8,128)(2,1)S(1)} all-to-all(bf16[4,80,384]{2,1,0:T(8,128)(2,1)S(1)} %broadcast_in_dim.44), channel_id=1, replica_groups=mesh['role'=2,'dp_0'=4,'dp_1'=4,'mp_0'=4,'mp_1'=2] {'mp_0'}, dimensions={0} | all-to-all | bytes 491520 | tf_op jit(solution)/shard_map/all_to_all | solution.py:30
  196.9 0.8 collective-permute-done.4
  202.0 0.7 fusion.84
  202.8 1.3 fusion.19
  204.2 1.0 copy.71
  205.1 4.9 %all-to-all-start.8 = ((bf16[4,384,160]{1,2,0:T(8,128)(2,1)}), bf16[4,384,160]{1,2,0:T(8,128)(2,1)S(1)}, u32[]{:S(2)}, u32[]{:S(2)}) async-start(bf16[4,384,160]{1,2,0:T(8,128)(2,1)} %bitcast.26), calls=%async_computation.8 | async-start | bytes 983040 | tf_op jit(solution)/shard_map/all_to_all | solution.py:34
  210.4 1.8 convolution_convert_fusion.1
  212.2 6.1 %all-to-all-done.8 = bf16[4,384,160]{1,2,0:T(8,128)(2,1)S(1)} async-done(((bf16[4,384,160]{1,2,0:T(8,128)(2,1)}), bf16[4,384,160]{1,2,0:T(8,128)(2,1)S(1)}, u32[]{:S(2)}, u32[]{:S(2)}) %all-to-all-start.8) | async-done | bytes 491552 | tf_op jit(solution)/shard_map/all_to_all | solution.py:34
  218.9 24.4 %all_to_all.51 = bf16[32,12,640]{2,1,0:T(8,128)(2,1)S(1)} all-to-all(bf16[32,12,640]{2,1,0:T(8,128)(2,1)S(1)} %reshape.183), channel_id=1, replica_groups=mesh['role'=2,'dp_0'=4,'dp_1'=4,'mp_0'=4,'mp_1'=2] {'role','dp_0','dp_1'}, dimensions={0} | all-to-all | bytes 983040 | tf_op jit(solution)/shard_map/all_to_all | solution.py:34
  (101 shorter events, 10.6 us)
Async XLA Ops:
  0.6 1.1 copy-start
  1.7 8.2 %copy-start.15 = (bf16[12,160]{1,0:T(8,128)(2,1)S(1)}, bf16[12,160]{1,0:T(8,128)(2,1)}, u32[]{:S(2)}) copy-start(bf16[12,160]{1,0:T(8,128)(2,1)} %param.18) | copy-start | bytes 11524
  1.7 8.2 %copy-start.16 = (bf16[192,12]{0,1:T(8,128)(2,1)S(1)}, bf16[192,12]{0,1:T(8,128)(2,1)}, u32[]{:S(2)}) copy-start(bf16[192,12]{0,1:T(8,128)(2,1)} %param.17) | copy-start | bytes 13828
  1.7 8.2 %copy-start.17 = (bf16[12,192]{1,0:T(8,128)(2,1)S(1)}, bf16[12,192]{1,0:T(8,128)(2,1)}, u32[]{:S(2)}) copy-start(bf16[12,192]{1,0:T(8,128)(2,1)} %param.16) | copy-start | bytes 13828
  3.3 26.8 %copy-start.13 = (bf16[640,40]{0,1:T(8,128)(2,1)S(1)}, bf16[640,40]{0,1:T(8,128)(2,1)}, u32[]{:S(2)}) copy-start(bf16[640,40]{0,1:T(8,128)(2,1)} %param.15) | copy-start | bytes 153604
  3.3 26.8 %copy-start.14 = (bf16[40,640]{1,0:T(8,128)(2,1)S(1)}, bf16[40,640]{1,0:T(8,128)(2,1)}, u32[]{:S(2)}) copy-start(bf16[40,640]{1,0:T(8,128)(2,1)} %param.14) | copy-start | bytes 153604
  3.3 14.4 %all-to-all-start.3 = ((bf16[4,160,512]{2,1,0:T(8,128)(2,1)}), bf16[4,160,512]{2,1,0:T(8,128)(2,1)S(1)}, u32[]{:S(2)}, u32[]{:S(2)}) async-start(bf16[4,160,512]{2,1,0:T(8,128)(2,1)} %broadcast_in_dim.19), calls=%async_computation.3 | async-start | bytes 1310720 | tf_op jit(solution)/shard_map/all_to_all | solution.py:30
  18.6 31.6 %all-to-all-start = ((bf16[32,12,640]{2,1,0:T(8,128)(2,1)}), bf16[32,12,640]{2,1,0:T(8,128)(2,1)S(1)}, u32[]{:S(2)}, u32[]{:S(2)}) async-start(bf16[32,12,640]{2,1,0:T(8,128)(2,1)} %broadcast_in_dim.17), calls=%async_computation | async-start | bytes 1310720 | tf_op jit(solution)/shard_map/all_to_all | solution.py:30
  50.2 35.0 %copy-start.2 = (bf16[32,12,640]{2,1,0:T(8,128)(2,1)}, bf16[32,12,640]{2,1,0:T(8,128)(2,1)S(1)}, u32[]{:S(2)}) copy-start(bf16[32,12,640]{2,1,0:T(8,128)(2,1)S(1)} %all-to-all-done) | copy-start | bytes 1474564
  51.2 24.9 %all-to-all-start.4 = ((bf16[8,80,640]{2,1,0:T(8,128)(2,1)}), bf16[8,80,640]{2,1,0:T(8,128)(2,1)S(1)}, u32[]{:S(2)}, u32[]{:S(2)}) async-start(bf16[8,80,640]{2,1,0:T(8,128)(2,1)} %broadcast_in_dim.20), calls=%async_computation.4 | async-start | bytes 1638400 | tf_op jit(solution)/shard_map/all_to_all | solution.py:30
  78.1 41.2 %all-to-all-start.5 = ((bf16[4,640,640]{2,1,0:T(8,128)(2,1)}), bf16[4,640,640]{2,1,0:T(8,128)(2,1)}, u32[]{:S(2)}, u32[]{:S(2)}) async-start(bf16[4,640,640]{2,1,0:T(8,128)(2,1)} %broadcast_in_dim.21), calls=%async_computation.5 | async-start | bytes 6553600 | tf_op jit(solution)/shard_map/all_to_all | solution.py:30
  83.8 2.7 %copy-start.3 = (bf16[256,384]{1,0:T(8,128)(2,1)}, bf16[256,384]{1,0:T(8,128)(2,1)S(1)}, u32[]{:S(2)}) copy-start(bf16[256,384]{1,0:T(8,128)(2,1)S(1)} %get-tuple-element.26) | copy-start | bytes 589828
  83.9 2.7 %copy-start.5 = (bf16[256,384]{1,0:T(8,128)(2,1)}, bf16[256,384]{1,0:T(8,128)(2,1)S(1)}, u32[]{:S(2)}) copy-start(bf16[256,384]{1,0:T(8,128)(2,1)S(1)} %get-tuple-element.27) | copy-start | bytes 589828
  84.6 4.6 %collective-permute-start.2 = (bf16[640,512]{0,1:T(8,128)(2,1)S(1)}, bf16[640,512]{0,1:T(8,128)(2,1)S(1)}, u32[]{:S(2)}, u32[]{:S(2)}) collective-permute-start(bf16[640,512]{0,1:T(8,128)(2,1)S(1)} %copy.67), channel_id=1, source_target_pairs={{0,1},{1,0},{2,3},{3,2},{4,5},{5,4},{6,7},{7,6},{8,9},{9,8},{10,11... | collective-permute-start | bytes 1966088 | tf_op jit(solution)/shard_map/ppermute | solution.py:38
  85.4 3.3 %copy-start.7 = (bf16[384,640]{1,0:T(8,128)(2,1)}, bf16[384,640]{1,0:T(8,128)(2,1)S(1)}, u32[]{:S(2)}) copy-start(bf16[384,640]{1,0:T(8,128)(2,1)S(1)} %reshape.171) | copy-start | bytes 1474564
  86.6 2.7 %copy-start.10 = (f32[512,192]{0,1:T(8,128)}, f32[512,192]{0,1:T(8,128)S(1)}, u32[]{:S(2)}) copy-start(f32[512,192]{0,1:T(8,128)S(1)} %fusion.54) | copy-start | bytes 1179652
  87.0 0.9 copy-start.1
  88.7 46.9 %collective-permute-start = (f32[256,384]{1,0:T(8,128)}, f32[256,384]{1,0:T(8,128)}, u32[]{:S(2)}, u32[]{:S(2)}) collective-permute-start(f32[256,384]{1,0:T(8,128)} %slice.109), channel_id=1, source_target_pairs={{0,1},{1,0},{2,3},{3,2},{4,5},{5,4},{6,7},{7,6},{8,9},{9,8},{10,11... | collective-permute-start | bytes 1179656 | tf_op jit(solution)/shard_map/ppermute | solution.py:38
  123.3 1.8 copy-start.9
  125.1 34.9 %collective-permute-start.3 = (f32[256,1280]{1,0:T(8,128)}, f32[256,1280]{1,0:T(8,128)}, u32[]{:S(2)}, u32[]{:S(2)}) collective-permute-start(f32[256,1280]{1,0:T(8,128)} %fusion.51), channel_id=1, source_target_pairs={{0,1},{1,0},{2,3},{3,2},{4,5},{5,4},{6,7},{7,6},{8,9},{9,8},{10,11... | collective-permute-start | bytes 3932168 | tf_op jit(solution)/shard_map/ppermute | solution.py:38
  130.1 14.3 %all-to-all-start.2 = ((bf16[4,384,160]{1,2,0:T(8,128)(2,1)}), bf16[4,384,160]{1,2,0:T(8,128)(2,1)}, u32[]{:S(2)}, u32[]{:S(2)}) async-start(bf16[4,384,160]{1,2,0:T(8,128)(2,1)} %broadcast_in_dim.18), calls=%async_computation.2 | async-start | bytes 983040 | tf_op jit(solution)/shard_map/all_to_all | solution.py:30
  144.4 12.3 %all-to-all-start.1 = ((f32[4,64,384]{2,1,0:T(8,128)}), f32[4,64,384]{2,1,0:T(8,128)}, u32[]{:S(2)}, u32[]{:S(2)}) async-start(f32[4,64,384]{2,1,0:T(8,128)} %bitcast.59), calls=%async_computation.1 | async-start | bytes 786432 | tf_op jit(solution)/shard_map/all_to_all | solution.py:34
  152.7 24.1 %collective-permute-start.1 = (bf16[384,640]{0,1:T(8,128)(2,1)}, bf16[384,640]{0,1:T(8,128)(2,1)}, u32[]{:S(2)}, u32[]{:S(2)}) collective-permute-start(bf16[384,640]{0,1:T(8,128)(2,1)} %bitcast.4), channel_id=1, source_target_pairs={{0,1},{1,0},{2,3},{3,2},{4,5},{5,4},{6,7},{7,6},{8,9},{9,8},{10,11... | collective-permute-start | bytes 1474568 | tf_op jit(solution)/shard_map/ppermute | solution.py:38
  163.1 13.3 %all-to-all-start.6 = ((bf16[4,64,1280]{2,1,0:T(8,128)(2,1)}), bf16[4,64,1280]{2,1,0:T(8,128)(2,1)S(1)}, u32[]{:S(2)}, u32[]{:S(2)}) async-start(bf16[4,64,1280]{2,1,0:T(8,128)(2,1)} %bitcast.57), calls=%async_computation.6 | async-start | bytes 1310720 | tf_op jit(solution)/shard_map/all_to_all | solution.py:34
  176.8 6.1 %copy-start.8 = (f32[64,384]{1,0:T(8,128)S(1)}, f32[64,384]{1,0:T(8,128)}, u32[]{:S(2)}) copy-start(f32[64,384]{1,0:T(8,128)} %get-tuple-element.21) | copy-start | bytes 294916
  179.5 5.4 %copy-start.12 = (bf16[64,1280]{1,0:T(8,128)(2,1)}, bf16[64,1280]{1,0:T(8,128)(2,1)S(1)}, u32[]{:S(2)}) copy-start(bf16[64,1280]{1,0:T(8,128)(2,1)S(1)} %get-tuple-element.31) | copy-start | bytes 491524
  185.4 17.4 %collective-permute-start.5 = (f32[384,640]{1,0:T(8,128)S(1)}, f32[384,640]{1,0:T(8,128)S(1)}, u32[]{:S(2)}, u32[]{:S(2)}) collective-permute-start(f32[384,640]{1,0:T(8,128)S(1)} %fusion.67), channel_id=1, source_target_pairs={{0,1},{1,0},{2,3},{3,2},{4,5},{5,4},{6,7},{7,6},{8,9},{9,8},{10,11... | collective-permute-start | bytes 2949128 | tf_op jit(solution)/shard_map/ppermute | solution.py:38
  196.1 1.5 collective-permute-start.4
  202.8 7.2 %copy-start.11 = (f32[512,192]{0,1:T(8,128)S(1)}, f32[512,192]{0,1:T(8,128)}, u32[]{:S(2)}) copy-start(f32[512,192]{0,1:T(8,128)} %copy-done.10) | copy-start | bytes 1179652
  204.1 6.2 %copy-start.4 = (bf16[256,384]{1,0:T(8,128)(2,1)S(1)}, bf16[256,384]{1,0:T(8,128)(2,1)}, u32[]{:S(2)}) copy-start(bf16[256,384]{1,0:T(8,128)(2,1)} %copy-done.3) | copy-start | bytes 589828
  204.1 6.2 %copy-start.6 = (bf16[256,384]{1,0:T(8,128)(2,1)S(1)}, bf16[256,384]{1,0:T(8,128)(2,1)}, u32[]{:S(2)}) copy-start(bf16[256,384]{1,0:T(8,128)(2,1)} %copy-done.5) | copy-start | bytes 589828
  204.1 6.2 %copy-start.18 = (f32[512]{0:T(512)S(1)}, f32[512]{0:T(512)}, u32[]{:S(2)}) copy-start(f32[512]{0:T(512)} %add_rsqrt_fusion.1) | copy-start | bytes 6148
  205.1 13.1 %all-to-all-start.8 = ((bf16[4,384,160]{1,2,0:T(8,128)(2,1)}), bf16[4,384,160]{1,2,0:T(8,128)(2,1)S(1)}, u32[]{:S(2)}, u32[]{:S(2)}) async-start(bf16[4,384,160]{1,2,0:T(8,128)(2,1)} %bitcast.26), calls=%async_computation.8 | async-start | bytes 983040 | tf_op jit(solution)/shard_map/all_to_all | solution.py:34
